TPU v7x, 256 devices: a whole 4x4x8 slice. The times are simulated.
256 devices in a mesh: dp: 32 (over z, x), heads: 8 (over y, core).
Axes of the slice: x: 4, y: 4, z: 8, core: 2. Of those that a mesh axis runs over, the one named last changes fastest.
Arguments:
- queries: bfloat16 [256, 16, 128], P('dp', 'heads'), may hold values from -12 to 12
- key_cache: bfloat16 [2048, 8, 256, 128], P('dp', 'heads'), may hold values from -6 to 6
- value_cache: bfloat16 [2048, 8, 256, 128], P('dp', 'heads'), may hold values from -6 to 6
- lengths_seen: int32 [256, 8], P('dp', 'heads'), may hold values from 1025 to 2048, as said below
- page_table: int32 [256, 8], P('dp'), may hold values from 0 to 63, as said below
- finished: int32 [256], P('dp'), may hold values from 0 to 1, as said below
- move_plan: int32 [1024, 3], P('dp'), may hold values from 0 to 63, as said below
Outputs:
- attention: bfloat16 [256, 16, 128], P('dp', 'heads')
Inputs may be any that keep to these rules, and one draw needn't show every extreme that they name: `lengths_seen`: each session's length, the largest entry of its row, lies between (5) * 256 + 1 and 2048. `page_table`: the 8 rows of one device's sessions hold each of that device's slot numbers exactly once. At most 2 sessions of one device are finished. `move_plan`: A row's source device differs from its receiving device; the destination slots of one receiving device are distinct, and each holds, after the moves, a page below the length of a session that is not finished. One device receives at most 2 pages from one source device, and on every device some source sends exactly 2.
All inputs are finite; a program needn't handle non-finite values.
Results may differ from a plain program's by a relative error of at most 0.008.
Values may be sent and summed in bfloat16 or wider, within the bound.
A program may use at most 64 MiB of HBM per device.

v0:
```python
import math

import jax
import jax.numpy as jnp
from jax import lax
from jax.sharding import PartitionSpec as P

softcap_limit = 50.0
score_divisor = 12.0


def from_everyone(array, axis):
    copies = jnp.broadcast_to(array, (lax.axis_size(axis), *array.shape))
    return lax.all_to_all(copies, axis, split_axis=0, concat_axis=0, tiled=True)


def taken_together(array, axis):
    everything = from_everyone(array, axis)
    return jnp.max(everything, axis=0)


def sent_together(arrays, axis, split_dim, concat_dim, along):
    widths = [a.shape[along] for a in arrays]
    both = jnp.concatenate(arrays, axis=along)
    filled = lax.all_to_all(both, axis, split_axis=split_dim, concat_axis=concat_dim, tiled=True)
    return tuple(jnp.split(filled, [sum(widths[:k]) for k in range(1, len(widths))], axis=along))


def in_one_piece(arrays, axis, split_dim, concat_dim, along):
    widths = [math.prod(a.shape[along:]) for a in arrays]
    both = jnp.concatenate(
        [a.reshape(*a.shape[:along], w) for a, w in zip(arrays, widths)], axis=along
    )
    filled = lax.all_to_all(both, axis, split_axis=split_dim, concat_axis=concat_dim, tiled=True)
    pieces = jnp.split(filled, [sum(widths[:k]) for k in range(1, len(widths))], axis=along)
    return tuple(
        (b.reshape(*filled.shape[:along], *a.shape[along:]) for a, b in zip(arrays, pieces))
    )


def page_terms(query_rows, key_rows, value_rows, live_counts):
    raw_scores = (
        jnp.einsum("nkgd,nktd->nkgt", query_rows, key_rows, preferred_element_type=jnp.float32)
        / score_divisor
    )
    capped = softcap_limit * jnp.tanh(raw_scores / softcap_limit)
    places = lax.broadcasted_iota(jnp.int32, capped.shape, 3)
    weights = jnp.where(
        places < live_counts[:, None, None, None], jnp.exp(capped), jnp.float32(0.0)
    ).astype(jnp.bfloat16)
    numerator = jnp.einsum(
        "nkgt,nktd->nkgd", weights, value_rows, preferred_element_type=jnp.float32
    )
    denominator = jnp.sum(weights.astype(jnp.float32), axis=3)
    return (numerator, denominator)


def body(queries, key_cache, value_cache, lengths_seen, page_table, finished, move_plan):
    slot_total, kv_heads, page_size, head_dim = key_cache.shape
    sessions, q_heads, _ = queries.shape
    group_size = q_heads // kv_heads
    pages_max = page_table.shape[1]
    move_count = move_plan.shape[0]
    peer_count = lax.axis_size("dp")
    capacity = (move_count - 1) // (peer_count - 1) + 1
    highest = lax.Precision.HIGHEST
    lengths = taken_together(jnp.max(lengths_seen, axis=1), "heads")
    entry_ids = jnp.arange(sessions * pages_max, dtype=jnp.int32)
    slot_ids = jnp.arange(slot_total, dtype=jnp.int32)
    flat_table = page_table.reshape(-1)
    owner_table = flat_table[None, :] == slot_ids[:, None]
    slot_entry = jnp.sum(jnp.where(owner_table, entry_ids[None, :], 0), axis=1)
    slot_session = slot_entry // pages_max
    slot_page = slot_entry % pages_max
    session_hot = slot_session[None, :] == jnp.arange(sessions, dtype=jnp.int32)[:, None]
    slot_length = jnp.sum(jnp.where(session_hot, lengths[:, None], 0), axis=0)
    slot_valid = jnp.clip(slot_length - slot_page * page_size, 0, page_size)
    source_device = move_plan[:, 0]
    source_slot = move_plan[:, 1]
    destination = move_plan[:, 2]
    dest_hot = destination[:, None] == slot_ids[None, :]
    moved_in = jnp.any(dest_hot, axis=0)
    local_valid = jnp.where(moved_in, 0, slot_valid)
    flat_queries = queries.reshape(sessions, kv_heads * group_size * head_dim)
    selector = session_hot.T.astype(jnp.bfloat16)
    slot_queries = jnp.dot(selector, flat_queries, preferred_element_type=jnp.float32).astype(
        jnp.bfloat16
    )
    local_numerator, local_denominator = page_terms(
        slot_queries.reshape(slot_total, kv_heads, group_size, head_dim),
        key_cache,
        value_cache,
        local_valid,
    )
    row_ids = jnp.arange(move_count, dtype=jnp.int32)
    earlier = (source_device[None, :] == source_device[:, None]) & (
        row_ids[None, :] < row_ids[:, None]
    )
    send_rank = jnp.sum(earlier.astype(jnp.int32), axis=1)
    buffer_place = source_device * capacity + send_rank
    place_hot = buffer_place[:, None] == jnp.arange(peer_count * capacity, dtype=jnp.int32)[None, :]
    row_session = jnp.sum(jnp.where(dest_hot, slot_session[None, :], 0), axis=1)
    row_valid = jnp.sum(jnp.where(dest_hot, slot_valid[None, :], 0), axis=1)
    row_queries = jnp.dot(
        dest_hot.astype(jnp.bfloat16), slot_queries, preferred_element_type=jnp.float32
    ).astype(jnp.bfloat16)
    request_slot = jnp.sum(jnp.where(place_hot, source_slot[:, None], 0), axis=0).reshape(
        peer_count, capacity
    )
    carry_hot = place_hot.T.astype(jnp.bfloat16)
    request_query = jnp.dot(carry_hot, row_queries, preferred_element_type=jnp.float32).astype(
        jnp.bfloat16
    )
    request_query = request_query.reshape(peer_count, capacity, kv_heads, group_size, head_dim)
    request_valid = jnp.sum(jnp.where(place_hot, row_valid[:, None], 0), axis=0).reshape(
        peer_count, capacity
    )
    asked_slot, asked_valid, asked_query = (
        *sent_together((request_slot, request_valid), "dp", 0, 0, 1),
        lax.all_to_all(request_query, "dp", split_axis=0, concat_axis=0, tiled=True),
    )
    flat_asked = asked_slot.reshape(-1)
    part_numerator, part_denominator = page_terms(
        asked_query.reshape(peer_count * capacity, kv_heads, group_size, head_dim),
        key_cache[flat_asked],
        value_cache[flat_asked],
        asked_valid.reshape(-1),
    )
    back_numerator, back_denominator = in_one_piece(
        (
            part_numerator.reshape(peer_count, capacity, kv_heads, group_size, head_dim),
            part_denominator.reshape(peer_count, capacity, kv_heads, group_size),
        ),
        "dp",
        0,
        0,
        4,
    )
    row_numerator = back_numerator.reshape(peer_count * capacity, kv_heads, group_size, head_dim)[
        buffer_place
    ]
    row_denominator = back_denominator.reshape(peer_count * capacity, kv_heads, group_size)[
        buffer_place
    ]
    session_float = session_hot.astype(jnp.float32)
    row_hot = (row_session[None, :] == jnp.arange(sessions, dtype=jnp.int32)[:, None]).astype(
        jnp.float32
    )
    numerator = jnp.dot(session_float, local_numerator.reshape(slot_total, -1), precision=highest)
    numerator = numerator + jnp.dot(
        row_hot, row_numerator.reshape(move_count, -1), precision=highest
    )
    denominator = jnp.dot(
        session_float, local_denominator.reshape(slot_total, -1), precision=highest
    )
    denominator = denominator + jnp.dot(
        row_hot, row_denominator.reshape(move_count, -1), precision=highest
    )
    output = numerator.reshape(sessions, q_heads, head_dim) / denominator[:, :, None]
    output = jnp.where(finished[:, None, None] == 1, jnp.float32(0.0), output)
    return output.astype(jnp.bfloat16)


def solution(mesh):
    in_specs = (
        P("dp", "heads", None),
        P("dp", "heads", None, None),
        P("dp", "heads", None, None),
        P("dp", "heads"),
        P("dp", None),
        P("dp"),
        P("dp", None),
    )
    out_specs = P("dp", "heads", None)
    return jax.shard_map(body, mesh=mesh, in_specs=in_specs, out_specs=out_specs, check_vma=False)
```

profile of v0, /device:TPU:8, one launch (start us, length us, event | category | flops | bytes accessed | tf_op | source)
XLA Modules:
  0.0 79.8 jit_solution(1657596636325088966)
XLA Ops:
  0.0 1.2 %broadcast_in_dim.111 = s32[8,1,8]{2,1,0:T(1,128)} broadcast(s32[8]{0:T(128)} %bitcast.74), dimensions={2} | broadcast | bytes 288 | tf_op jit(solution)/shard_map/broadcast_in_dim | solution.py:13
  1.2 5.4 %all-to-all-start = ((s32[8,1,8]{2,1,0:T(1,128)}), s32[8,1,8]{2,1,0:T(1,128)S(1)}, u32[]{:S(2)}, u32[]{:S(2)}) async-start(s32[8,1,8]{2,1,0:T(1,128)} %broadcast_in_dim.111), calls=%async_computation | async-start | bytes 8192 | tf_op jit(solution)/shard_map/all_to_all | solution.py:14
  6.6 0.8 eq.93
  7.4 0.1 select_reduce_fusion
  7.5 0.7 slice_bitcast_fusion.2
  8.2 0.2 convert_reduce_fusion.2
  8.4 0.8 %fusion.34 = (s32[32]{0:T(128)S(1)}, s32[32]{0:T(128)S(1)}, s32[32]{0:T(128)S(1)}, s32[32]{0:T(128)S(1)}) fusion(s32[32]{0:T(128)S(1)} %convert_reduce_fusion.2, s32[32,3]{0,1:T(4,128)} %param.13), kind=kLoop, calls=%fused_computation.72 | loop fusion | flops 160 | bytes 1024 | tf_op jit(solution)/shard_map/select_n | solution.py:139
  9.2 0.1 fusion.16
  9.3 0.7 broadcast_compare_fusion
  9.9 0.9 %convolution_convert_fusion = bf16[64,256]{1,0:T(8,128)(2,1)S(1)} fusion(bf16[1,8,2,128]{3,2,1,0:T(2,128)(2,1)} %bitcast.73, s32[64]{0:T(128)S(1)} %and_select_fusion.1), kind=kOutput, calls=%fused_computation.16 | convolution fusion | flops 279040 | bytes 37120 | tf_op jit(solution)/shard_map/dot_general | solution.py:86
  10.8 0.3 convolution_convert_fusion.1
  11.2 0.6 reshape.206
  11.8 0.1 select_reduce_fusion.5
  11.9 0.2 select_reduce_fusion.4
  12.1 0.1 select_reduce_fusion.3
  12.2 0.1 reshape.204
  12.3 0.1 copy.58
  12.4 0.1 reshape.205
  12.5 0.1 copy.59
  12.6 0.7 copy.60
  13.3 10.9 %all-to-all-start.1 = ((s32[32,1,4]{2,1,0:T(1,128)}), s32[32,1,4]{2,1,0:T(1,128)S(1)}, u32[]{:S(2)}, u32[]{:S(2)}) async-start(s32[32,1,4]{2,1,0:T(1,128)} %copy.60), calls=%async_computation.1 | async-start | bytes 32768 | tf_op jit(solution)/shard_map/all_to_all | solution.py:25
  24.2 0.0 copy-start
  24.2 3.6 %convert_reduce_fusion = (f32[64,2]{1,0:T(8,128)S(1)}, bf16[64,2,256]{2,1,0:T(2,128)(2,1)S(1)}) fusion(bf16[64,2,128]{2,1,0:T(2,128)(2,1)S(1)} %reshape.200, bf16[64,1,256,128]{3,2,1,0:T(8,128)(2,1)} %param.8, s32[64]{0:T(128)S(1)} %get-tuple-element.9), kind=kOutput, calls=%fused_computation.23 | convolution fusion | flops 8617856 | bytes 4293376 | tf_op jit(solution)/shard_map/nkgd,nktd->nkgt/dot_general | solution.py:43
  27.8 0.7 fusion.36
  28.5 0.1 fusion.11
  28.6 5.2 %all-to-all-done.1 = s32[32,1,4]{2,1,0:T(1,128)S(1)} async-done(((s32[32,1,4]{2,1,0:T(1,128)}), s32[32,1,4]{2,1,0:T(1,128)S(1)}, u32[]{:S(2)}, u32[]{:S(2)}) %all-to-all-start.1) | async-done | bytes 544 | tf_op jit(solution)/shard_map/all_to_all | solution.py:25
  33.8 4.6 %all-to-all-start.2 = ((bf16[32,2,1,2,128]{4,3,1,2,0:T(2,128)(2,1)}), bf16[32,2,1,2,128]{4,3,1,2,0:T(2,128)(2,1)S(1)}, u32[]{:S(2)}, u32[]{:S(2)}) async-start(bf16[32,2,1,2,128]{4,3,1,2,0:T(2,128)(2,1)} %bitcast.11), calls=%async_computation.2 | async-start | bytes 65536 | tf_op jit(solution)/shard_map/all_to_all | solution.py:120
  38.4 0.1 copy.61
  38.5 0.1 copy.64
  38.6 0.1 reshape.208
  38.7 0.1 copy.62
  38.8 0.1 lt.61
  38.9 5.2 %gather_fusion = bf16[64,256,128]{2,1,0:T(8,128)(2,1)} fusion(bf16[64,256,128]{2,1,0:T(8,128)(2,1)} %bitcast.62, s32[1024]{0:T(1024)S(1)} %pad_clamp_fusion.1), kind=kCustom, calls=%fused_computation | custom fusion | bytes 8388864 | tf_op jit(solution)/shard_map/gather | solution.py:125
  44.1 5.2 %gather_fusion.1 = bf16[64,256,128]{2,1,0:T(8,128)(2,1)} fusion(bf16[64,256,128]{2,1,0:T(8,128)(2,1)} %bitcast.63, s32[1024]{0:T(1024)S(1)} %pad_clamp_fusion.1), kind=kCustom, calls=%fused_computation.1 | custom fusion | bytes 8388864 | tf_op jit(solution)/shard_map/gather | solution.py:126
  49.3 3.5 %convert_reduce_fusion.1 = (f32[64,2]{1,0:T(8,128)S(1)}, bf16[64,2,256]{2,1,0:T(2,128)(2,1)S(1)}) fusion(bf16[64,2,128]{2,1,0:T(2,128)(2,1)S(1)} %bitcast.69, bf16[64,256,128]{2,1,0:T(8,128)(2,1)} %gather_fusion, s32[64]{0:T(128)S(1)} %lt.61), kind=kOutput, calls=%fused_computation.24 | convolution fusion | flops 8617856 | bytes 4293376 | tf_op jit(solution)/shard_map/nkgd,nktd->nkgt/dot_general | solution.py:43
  52.8 0.5 copy.67
  53.3 2.8 %fusion.42 = f32[64,2,128]{2,1,0:T(2,128)S(1)} fusion(bf16[64,2,256]{2,1,0:T(2,128)(2,1)S(1)} %get-tuple-element.18, bf16[64,256,128]{2,1,0:T(8,128)(2,1)} %gather_fusion.1), kind=kOutput, calls=%fused_computation.85 | convolution fusion | flops 8388608 | bytes 4325376 | tf_op jit(solution)/shard_map/nkgt,nktd->nkgd/dot_general | solution.py:51
  56.2 0.7 pad_maximum_fusion
  56.9 9.8 %all-to-all-start.3 = ((f32[32,2,1,2,129]{4,3,2,1,0:T(2,128)}), f32[32,2,1,2,129]{4,3,2,1,0:T(2,128)S(1)}, u32[]{:S(2)}, u32[]{:S(2)}) async-start(f32[32,2,1,2,129]{4,3,2,1,0:T(2,128)} %pad_maximum_fusion), calls=%async_computation.3 | async-start | bytes 262144 | tf_op jit(solution)/shard_map/all_to_all | solution.py:34
  66.7 0.2 fusion.25
  66.8 10.5 %all-to-all-done.3 = f32[32,2,1,2,129]{4,3,2,1,0:T(2,128)S(1)} async-done(((f32[32,2,1,2,129]{4,3,2,1,0:T(2,128)}), f32[32,2,1,2,129]{4,3,2,1,0:T(2,128)S(1)}, u32[]{:S(2)}, u32[]{:S(2)}) %all-to-all-start.3) | async-done | bytes 66080 | tf_op jit(solution)/shard_map/all_to_all | solution.py:34
  77.3 0.2 slice_reduce_fusion
  77.5 0.6 gather_fusion.3
  78.0 0.2 convolution_add_fusion.1
  78.2 0.1 copy.72
  78.4 0.6 gather_fusion.2
  79.0 0.1 fusion.10
  79.1 0.7 fusion.22
  (13 shorter events, 0.1 us)
Async XLA Ops:
  1.2 10.6 %all-to-all-start = ((s32[8,1,8]{2,1,0:T(1,128)}), s32[8,1,8]{2,1,0:T(1,128)S(1)}, u32[]{:S(2)}, u32[]{:S(2)}) async-start(s32[8,1,8]{2,1,0:T(1,128)} %broadcast_in_dim.111), calls=%async_computation | async-start | bytes 8192 | tf_op jit(solution)/shard_map/all_to_all | solution.py:14
  13.3 20.5 %all-to-all-start.1 = ((s32[32,1,4]{2,1,0:T(1,128)}), s32[32,1,4]{2,1,0:T(1,128)S(1)}, u32[]{:S(2)}, u32[]{:S(2)}) async-start(s32[32,1,4]{2,1,0:T(1,128)} %copy.60), calls=%async_computation.1 | async-start | bytes 32768 | tf_op jit(solution)/shard_map/all_to_all | solution.py:25
  24.2 3.6 %copy-start = (bf16[64,1,256,128]{3,2,1,0:T(8,128)(2,1)S(1)}, bf16[64,1,256,128]{3,2,1,0:T(8,128)(2,1)}, u32[]{:S(2)}) copy-start(bf16[64,1,256,128]{3,2,1,0:T(8,128)(2,1)} %param.9) | copy-start | bytes 12582916
  33.8 15.6 %all-to-all-start.2 = ((bf16[32,2,1,2,128]{4,3,1,2,0:T(2,128)(2,1)}), bf16[32,2,1,2,128]{4,3,1,2,0:T(2,128)(2,1)S(1)}, u32[]{:S(2)}, u32[]{:S(2)}) async-start(bf16[32,2,1,2,128]{4,3,1,2,0:T(2,128)(2,1)} %bitcast.11), calls=%async_computation.2 | async-start | bytes 65536 | tf_op jit(solution)/shard_map/all_to_all | solution.py:120
  56.9 20.4 %all-to-all-start.3 = ((f32[32,2,1,2,129]{4,3,2,1,0:T(2,128)}), f32[32,2,1,2,129]{4,3,2,1,0:T(2,128)S(1)}, u32[]{:S(2)}, u32[]{:S(2)}) async-start(f32[32,2,1,2,129]{4,3,2,1,0:T(2,128)} %pad_maximum_fusion), calls=%async_computation.3 | async-start | bytes 262144 | tf_op jit(solution)/shard_map/all_to_all | solution.py:34
where the time goes:
time: 80.3 us; the launch traced here: 79.8 us
  starting transfers between devices  30.6 us (38%)
  local copies, waits for them, and re-layouts  17.3 us (22%)
  waiting for transfers between devices  15.6 us (19%)
  matrix products  12.4 us (15%)
  other arithmetic  3.68 us (5%)
    all_to_all x1, starting transfers between devices, sent_together(): lax.all_to_all(both, axis, split_axis=split_dim, concat_axis=concat_dim,...  10.9 us
    all_to_all x1, waiting for transfers between devices, in_one_piece(): lax.all_to_all(both, axis, split_axis=split_dim, concat_axis=concat_dim,...  10.5 us
    all_to_all x1, starting transfers between devices, in_one_piece(): lax.all_to_all(both, axis, split_axis=split_dim, concat_axis=concat_dim,...  9.77 us
    dot_general x2, matrix products, page_terms(): jnp.einsum('nkgd,nktd->nkgt', query_rows, key_rows, preferred_element_typ...  7.09 us
    all_to_all x1, starting transfers between devices, from_everyone(): return lax.all_to_all(copies, axis, split_axis=0, concat_axis=0, tiled=True)  5.38 us
    gather x1, local copies, waits for them, and re-layouts, body(): value_cache[flat_asked]  5.24 us
    gather x1, local copies, waits for them, and re-layouts, body(): key_cache[flat_asked]  5.2 us
    all_to_all x1, waiting for transfers between devices, sent_together(): lax.all_to_all(both, axis, split_axis=split_dim, concat_axis=concat_dim,...  5.17 us
  transfers between devices with their start and end apart: 4, of which 2 were waited for; matrix products, arithmetic and copies ran while one was open for 26% of the time, Pallas kernels for 0%

commit v1 on v0

v1 whole, which is shorter than its diff:
```python
import functools

import jax
import jax.numpy as jnp
from jax import lax
from jax.experimental import pallas as pl
from jax.experimental.pallas import tpu as pltpu
from jax.sharding import PartitionSpec as P

NZ, NX = 8, 4
MESH = pl.DeviceIdType.MESH
F32, BF16, I32 = jnp.float32, jnp.bfloat16, jnp.int32


def hops(o):
    z, x = o // NX, o % NX
    return min(z, NZ - z) + min(x, NX - x)


def opposite(o):
    z, x = o // NX, o % NX
    return ((NZ - z) % NZ) * NX + (NX - x) % NX


NEAR_FIRST = sorted(range(1, NZ * NX), key=hops)
FAR_FIRST = NEAR_FIRST[::-1]


def nt(a, b, precision=None):
    return lax.dot_general(
        a, b, (((1,), (1,)), ((), ())), precision=precision, preferred_element_type=F32
    )


def nn(a, b, precision=None):
    return lax.dot_general(
        a, b, (((1,), (0,)), ((), ())), precision=precision, preferred_element_type=F32
    )


def iota(shape, dim):
    return lax.broadcasted_iota(I32, shape, dim)


def kernel(
    n_dp, n_heads,
    table_s, q_ref, k_hbm, v_hbm, seen_ref, table_ref, fin_ref, plan_ref,
    out_ref,
    k_buf, v_buf, ask_q, ask_w, got_q, got_w, len_out, len_in, len_max, got_len,
    e_loc, e_far, give, back,
    kv_sem, h_send, h_recv, q_send, q_recv, w_send, w_recv, l_send, l_recv, b_send, b_recv,
):
    me, head = lax.axis_index("dp"), lax.axis_index("heads")
    mz, mx = me // NX, lax.rem(me, NX)

    def peer(o):
        z, x = o // NX, o % NX
        return lax.rem(mz + z, NZ) * NX + lax.rem(mx + x, NX)

    def across(k):
        return lax.rem(head + k, n_heads)

    barrier = pltpu.get_barrier_semaphore()
    for o in FAR_FIRST:
        pl.semaphore_signal(barrier, inc=1, device_id={"dp": peer(o)}, device_id_type=MESH)
    for k in range(1, n_heads):
        pl.semaphore_signal(barrier, inc=1, device_id={"heads": across(k)}, device_id_type=MESH)

    k_copy = pltpu.make_async_copy(k_hbm, k_buf, kv_sem.at[0])
    v_copy = pltpu.make_async_copy(v_hbm, v_buf, kv_sem.at[1])
    k_copy.start()
    v_copy.start()

    src, slot, dest = plan_ref[0:1, :], plan_ref[1:2, :], plan_ref[2:3, :]
    rows = src.shape[1]
    off = ((src // NX - mz + NZ) % NZ) * NX + (src % NX - mx + NX) % NX
    sub, lane = iota((rows, rows), 0), iota((rows, rows), 1)
    off_f = off.astype(F32)
    off_col = jnp.sum(jnp.where(sub == lane, off_f, 0.0), axis=1, keepdims=True)
    same = (off_col == off_f) & (sub < lane)
    rank = jnp.sum(jnp.where(same, 1.0, 0.0), axis=0, keepdims=True)
    place = off_f * 2.0 + rank
    sub8 = iota((8, rows), 0)
    entry = jnp.zeros((8, rows), F32)
    for t in range(8):
        hit = table_ref[:, t : t + 1] == dest
        entry = entry + jnp.where(hit, (sub8 * 8 + t).astype(F32), 0.0)
    entry = jnp.sum(entry, axis=0, keepdims=True)
    session = jnp.floor(entry * 0.125)
    page = entry - session * 8.0

    hot16 = jnp.where((iota((16, rows), 0) // 2).astype(F32) == session, 1.0, 0.0).astype(BF16)
    n_back = n_dp * 8
    r8 = iota((n_back, rows), 0)
    lies = (r8 // 8 * 2 + (r8 % 8 // 2) % 2).astype(F32) == place
    spread = jnp.where(lies, 1.0, 0.0).astype(BF16)
    pick = nt(spread, hot16)
    row_a, col_a = iota((n_back, 16), 0), iota((n_back, 16), 1)
    pick = jnp.where((row_a % 2 == col_a % 2) & (row_a % 8 < 4), pick, 0.0).astype(BF16)
    q16 = q_ref[...].astype(F32).reshape(16, 128).astype(BF16)
    ask_q[...] = nn(pick, q16).reshape(n_dp, 8, 128).astype(BF16)
    word = slot.astype(F32) + 64.0 * session + 512.0 * page
    at = iota((n_dp, rows), 0).astype(F32) == off_f
    word_t = jnp.where(iota((128, rows), 0).astype(F32) == rank, word, 0.0)
    words = nt(jnp.where(at, 1.0, 0.0), word_t, lax.Precision.HIGHEST)
    ask_w[...] = words.astype(I32).reshape(n_dp, 1, 128)

    take = nt(hot16, spread)
    row_b, col_b = iota((16, n_back), 0), iota((16, n_back), 1)
    fits = row_b % 2 == col_b % 2
    take_num = jnp.where(fits & (col_b % 8 < 4), take, 0.0).astype(BF16)
    take_den = jnp.where(fits & (col_b % 8 >= 4), take, 0.0).astype(BF16)

    len_out[...] = jnp.zeros((1, 128), I32)
    len_out[0:1, 0:8] = seen_ref[...]
    len_in[0] = len_out[...]
    back[0] = jnp.zeros((8, 128), BF16)

    def weights(s):
        return jnp.exp(50.0 * jnp.tanh(s * (1.0 / 600.0)))

    row16 = iota((16, 128), 0) // 2
    k_copy.wait()
    for t in range(8):
        s = jnp.zeros((16, 256), F32)
        for n in range(8):
            mine = jnp.where(row16 == n, q16.astype(F32), 0.0).astype(BF16)
            s = s + nt(mine, k_buf[table_s[n, t]])
        e_loc[t] = weights(s)

    pl.semaphore_wait(barrier, n_dp - 1 + n_heads - 1)

    def h_copy(k):
        return pltpu.make_async_remote_copy(
            src_ref=len_out, dst_ref=len_in.at[n_heads - k],
            send_sem=h_send.at[k], recv_sem=h_recv.at[n_heads - k],
            device_id={"heads": across(k)}, device_id_type=MESH,
        )

    def dp_copy(src_ref, dst, send, recv, o):
        return pltpu.make_async_remote_copy(
            src_ref=src_ref, dst_ref=dst.at[opposite(o)],
            send_sem=send.at[o], recv_sem=recv.at[opposite(o)],
            device_id={"dp": peer(o)}, device_id_type=MESH,
        )

    def q_copy(o):
        return dp_copy(ask_q.at[o], got_q, q_send, q_recv, o)

    def w_copy(o):
        return dp_copy(ask_w.at[o], got_w, w_send, w_recv, o)

    def l_copy(o):
        return dp_copy(len_max, got_len, l_send, l_recv, o)

    def b_copy(o):
        return dp_copy(give.at[o], back, b_send, b_recv, o)

    for k in range(1, n_heads):
        h_copy(k).start()
    for o in FAR_FIRST:
        w_copy(o).start()
        q_copy(o).start()
    for k in range(1, n_heads):
        h_copy(n_heads - k).wait_recv()
    lengths = jnp.max(len_in[...], axis=0)
    len_max[...] = lengths
    for o in FAR_FIRST:
        l_copy(o).start()

    lens_f = lengths.astype(F32)
    r16, l16 = iota((16, 128), 0) // 2, iota((16, 128), 1)
    len_col = jnp.sum(jnp.where(r16 == l16, lens_f, 0.0), axis=1, keepdims=True)
    tok16 = iota((16, 256), 1).astype(F32)
    row16w = iota((16, 256), 0) // 2
    went = jnp.zeros((8, 8), F32)
    ent_row = entry
    hot8 = jnp.where((iota((16, rows), 0) // 2).astype(F32) == session, 1.0, 0.0)
    num = jnp.zeros((16, 128), F32)
    den = jnp.zeros((16, 256), F32)
    v_copy.wait()
    for t in range(8):
        moved = jnp.sum(jnp.where(page == float(t), hot8, 0.0), axis=1, keepdims=True)
        limit = jnp.where(moved > 0.0, 0.0, len_col - 256.0 * t)
        w = jnp.where(tok16 < limit, e_loc[t], 0.0).astype(BF16).astype(F32)
        den = den + w
        for n in range(8):
            mine = jnp.where(row16w == n, w, 0.0).astype(BF16)
            num = num + nn(mine, v_buf[table_s[n, t]])
    den = jnp.sum(den, axis=1, keepdims=True)

    row8 = iota((8, 128), 0)
    slots = {}
    for o in NEAR_FIRST:
        w_copy(opposite(o)).wait_recv()
        q_copy(opposite(o)).wait_recv()
        q8 = got_q[o].astype(F32)
        words_o = got_w[o]
        a, b = words_o[0, 0], words_o[0, 1]
        slots[o] = (a, b)
        s = nt(jnp.where(row8 < 2, q8, 0.0).astype(BF16), k_buf[a % 64])
        s = s + nt(jnp.where(row8 >= 2, q8, 0.0).astype(BF16), k_buf[b % 64])
        e_far[o] = weights(s)
    lane8 = iota((8, 128), 1)
    tok8, row8w = iota((8, 256), 1).astype(F32), iota((8, 256), 0)
    first = iota((8, 1), 0) < 2
    for o in NEAR_FIRST:
        a, b = slots[o]
        l_copy(opposite(o)).wait_recv()
        who = jnp.where(row8 < 2, a // 64 % 8, b // 64 % 8)
        part = jnp.where(first, a // 512 * 256, b // 512 * 256).astype(F32)
        length = jnp.sum(jnp.where(lane8 == who, got_len[o].astype(F32), 0.0), axis=1, keepdims=True)
        w = jnp.where(tok8 < length - part, e_far[o], 0.0).astype(BF16).astype(F32)
        d = jnp.sum(w, axis=1, keepdims=True)
        m = nn(jnp.where(row8w < 2, w, 0.0).astype(BF16), v_buf[a % 64])
        m = m + nn(jnp.where(row8w >= 2, w, 0.0).astype(BF16), v_buf[b % 64])
        d = jnp.broadcast_to(d, (8, 128))
        d = pltpu.roll(d, 4, 0)
        give[o] = jnp.where(row8 < 4, m, d).astype(BF16)
        b_copy(o).start()

    for o in NEAR_FIRST:
        b_copy(opposite(o)).wait_recv()
    got = back[...].astype(F32).reshape(n_back, 128).astype(BF16)
    num = num + nn(take_num, got)
    den = den + nn(take_den, got)
    live = jnp.sum(jnp.where(r16 == l16, fin16(fin_ref), 0.0), axis=1, keepdims=True)
    out_ref[...] = jnp.where(live == 1.0, 0.0, num / den).astype(BF16)

    for k in range(1, n_heads):
        h_copy(k).wait_send()
    for o in FAR_FIRST:
        w_copy(o).wait_send()
        q_copy(o).wait_send()
        l_copy(o).wait_send()
        b_copy(o).wait_send()


def fin16(fin_ref):
    row = fin_ref[...].astype(F32)
    return jnp.concatenate([row, jnp.zeros((1, 128 - row.shape[1]), F32)], axis=1)


def body(queries, key_cache, value_cache, lengths_seen, page_table, finished, move_plan):
    n_dp, n_heads = lax.axis_size("dp"), lax.axis_size("heads")
    slots, _, page, dim = key_cache.shape
    sessions, group, _ = queries.shape
    vmem = pl.BlockSpec(memory_space=pltpu.VMEM)
    hbm = pl.BlockSpec(memory_space=pl.ANY)
    dma = pltpu.SemaphoreType.DMA
    out = pl.pallas_call(
        functools.partial(kernel, n_dp, n_heads),
        out_shape=jax.ShapeDtypeStruct((sessions * group, dim), BF16),
        in_specs=[pl.BlockSpec(memory_space=pltpu.SMEM), vmem, hbm, hbm, vmem, vmem, vmem, vmem],
        out_specs=vmem,
        scratch_shapes=[
            pltpu.VMEM((slots, page, dim), BF16),
            pltpu.VMEM((slots, page, dim), BF16),
            pltpu.VMEM((n_dp, 8, dim), BF16),
            pltpu.VMEM((n_dp, 1, 128), I32),
            pltpu.VMEM((n_dp, 8, dim), BF16),
            pltpu.VMEM((n_dp, 1, 128), I32),
            pltpu.VMEM((1, 128), I32),
            pltpu.VMEM((n_heads, 1, 128), I32),
            pltpu.VMEM((1, 128), I32),
            pltpu.VMEM((n_dp, 1, 128), I32),
            pltpu.VMEM((8, 16, page), F32),
            pltpu.VMEM((n_dp, 8, page), F32),
            pltpu.VMEM((n_dp, 8, dim), BF16),
            pltpu.VMEM((n_dp, 8, dim), BF16),
            dma((2,)),
            dma((n_heads,)), dma((n_heads + 1,)),
            dma((n_dp,)), dma((n_dp,)),
            dma((n_dp,)), dma((n_dp,)),
            dma((n_dp,)), dma((n_dp,)),
            dma((n_dp,)), dma((n_dp,)),
        ],
        compiler_params=pltpu.CompilerParams(
            collective_id=0, has_side_effects=True, vmem_limit_bytes=48 << 20
        ),
        name="attend",
    )(
        page_table,
        queries,
        key_cache.reshape(slots, page, dim),
        value_cache.reshape(slots, page, dim),
        lengths_seen.reshape(1, sessions),
        page_table,
        finished.reshape(1, sessions),
        move_plan.T,
    )
    return out.reshape(sessions, group, dim)


def solution(mesh):
    in_specs = (
        P("dp", "heads", None),
        P("dp", "heads", None, None),
        P("dp", "heads", None, None),
        P("dp", "heads"),
        P("dp", None),
        P("dp"),
        P("dp", None),
    )
    out_specs = P("dp", "heads", None)
    return jax.shard_map(body, mesh=mesh, in_specs=in_specs, out_specs=out_specs, check_vma=False)
```

time: 80.3 us -> 45.7 us (0.57)
  the two profiles are of different devices: /device:TPU:8 before, /device:TPU:1 now
where the time goes in v1:
time: 45.7 us; the launch traced here: 45.4 us
  Pallas kernels  39.3 us (86%)
  local copies, waits for them, and re-layouts  6.15 us (13%)
    pallas_call x1, Pallas kernels, body(): pl.pallas_call(functools.partial(kernel, n_dp, n_heads), out_shape=jax.Sh...  39.3 us
    unnamed x13, local copies, waits for them, and re-layouts  6.15 us

profile of v1, /device:TPU:1, one launch (start us, length us, event | category | flops | bytes accessed | tf_op | source)
XLA Modules:
  0.0 45.4 jit_solution(4280266603577737454)
XLA Ops:
  0.0 0.0 copy-start
  0.0 2.2 %copy-done = bf16[64,1,256,128]{3,2,1,0:T(8,128)(2,1)S(1)} copy-done((bf16[64,1,256,128]{3,2,1,0:T(8,128)(2,1)S(1)}, bf16[64,1,256,128]{3,2,1,0:T(8,128)(2,1)}, u32[]{:S(2)}) %copy-start) | copy-done | bytes 4194328
  2.2 0.0 copy-start.1
  2.2 0.7 %copy-done.1 = s32[8,8]{1,0:T(8,128)S(1)} copy-done((s32[8,8]{1,0:T(8,128)S(1)}, s32[8,8]{1,0:T(8,128)}, u32[]{:S(2)}) %copy-start.1) | copy-done | bytes 280
  2.9 0.0 copy-start.2
  2.9 0.7 %copy-done.2 = bf16[8,2,128]{2,1,0:T(2,128)(2,1)S(1)} copy-done((bf16[8,2,128]{2,1,0:T(2,128)(2,1)S(1)}, bf16[8,2,128]{2,1,0:T(2,128)(2,1)}, u32[]{:S(2)}) %copy-start.2) | copy-done | bytes 4120
  3.6 0.0 copy-start.3
  3.6 0.7 %copy-done.3 = s32[32,3]{0,1:T(4,128)S(1)} copy-done((s32[32,3]{0,1:T(4,128)S(1)}, s32[32,3]{0,1:T(4,128)}, u32[]{:S(2)}) %copy-start.3) | copy-done | bytes 408
  4.2 0.0 copy-start.4
  4.2 0.7 %copy-done.4 = s32[8,1]{0,1:T(1,128)S(1)} copy-done((s32[8,1]{0,1:T(1,128)S(1)}, s32[8,1]{0,1:T(1,128)}, u32[]{:S(2)}) %copy-start.4) | copy-done | bytes 56
  4.9 0.0 copy-start.5
  4.9 0.7 %copy-done.5 = s32[8]{0:T(128)S(1)} copy-done((s32[8]{0:T(128)S(1)}, s32[8]{0:T(128)}, u32[]{:S(2)}) %copy-start.5) | copy-done | bytes 56
  5.6 39.3 %attend.1 = bf16[16,128]{1,0:T(8,128)(2,1)S(1)} custom-call(s32[8,8]{1,0:T(8,128)S(1)} %copy-done.1, bf16[8,2,128]{2,1,0:T(2,128)(2,1)S(1)} %copy-done.2, bf16[64,256,128]{2,1,0:T(8,128)(2,1)S(1)} %bitcast.6, bf16[64,256,128]{2,1,0:T(8,128)(2,1)} %bitcast.11, s32[1,8]{1,0:T(1,128)S(1)} %bitcast.9, s32[8,8]{1,0:T(8,128)S(1)} %copy-done.1, ...), custom_call_target="tpu_custom_call" | custom-call | tf_op jit(solution)/shard_map/attend/pallas_call | solution.py:251
  44.8 0.6 %copy.9 = bf16[8,2,128]{2,1,0:T(2,128)(2,1)} copy(bf16[8,2,128]{2,1,0:T(2,128)(2,1)S(1)} %bitcast.7) | data formatting | bytes 8192
Async XLA Ops:
  0.0 2.2 %copy-start = (bf16[64,1,256,128]{3,2,1,0:T(8,128)(2,1)S(1)}, bf16[64,1,256,128]{3,2,1,0:T(8,128)(2,1)}, u32[]{:S(2)}) copy-start(bf16[64,1,256,128]{3,2,1,0:T(8,128)(2,1)} %param.8) | copy-start | bytes 12582916
  2.2 0.7 %copy-start.1 = (s32[8,8]{1,0:T(8,128)S(1)}, s32[8,8]{1,0:T(8,128)}, u32[]{:S(2)}) copy-start(s32[8,8]{1,0:T(8,128)} %table_ref.1) | copy-start | bytes 772
  2.9 0.7 %copy-start.2 = (bf16[8,2,128]{2,1,0:T(2,128)(2,1)S(1)}, bf16[8,2,128]{2,1,0:T(2,128)(2,1)}, u32[]{:S(2)}) copy-start(bf16[8,2,128]{2,1,0:T(2,128)(2,1)} %q_ref.1) | copy-start | bytes 12292
  3.6 0.7 %copy-start.3 = (s32[32,3]{0,1:T(4,128)S(1)}, s32[32,3]{0,1:T(4,128)}, u32[]{:S(2)}) copy-start(s32[32,3]{0,1:T(4,128)} %param.13) | copy-start | bytes 1156
  4.2 0.7 %copy-start.4 = (s32[8,1]{0,1:T(1,128)S(1)}, s32[8,1]{0,1:T(1,128)}, u32[]{:S(2)}) copy-start(s32[8,1]{0,1:T(1,128)} %param.10) | copy-start | bytes 100
  4.9 0.7 %copy-start.5 = (s32[8]{0:T(128)S(1)}, s32[8]{0:T(128)}, u32[]{:S(2)}) copy-start(s32[8]{0:T(128)} %param.12) | copy-start | bytes 100

commit v2 on v1

v2 whole, which is shorter than its diff:
```python
import functools

import jax
import jax.numpy as jnp
from jax import lax
from jax.experimental import pallas as pl
from jax.experimental.pallas import tpu as pltpu
from jax.sharding import PartitionSpec as P

MESH = pl.DeviceIdType.MESH
F32, BF16, I32 = jnp.float32, jnp.bfloat16, jnp.int32
BATCH = 4


def nt(a, b, precision=None):
    return lax.dot_general(
        a, b, (((1,), (1,)), ((), ())), precision=precision, preferred_element_type=F32
    )


def nn(a, b, precision=None):
    return lax.dot_general(
        a, b, (((1,), (0,)), ((), ())), precision=precision, preferred_element_type=F32
    )


def iota(shape, dim):
    return lax.broadcasted_iota(I32, shape, dim)


def one_hot(mask):
    return jnp.where(mask, 1.0, 0.0).astype(BF16)


def weights(s):
    return jnp.exp(50.0 * jnp.tanh(s * (1.0 / 600.0)))


def kernel(
    n_dp, n_heads,
    q_hbm, k_hbm, v_hbm, seen_hbm, table_hbm, fin_hbm, plan_hbm,
    out_ref,
    q_ref, k_buf, v_buf, seen_ref, table_s, table_ref, fin_ref, plan_ref,
    ask_q, ask_w, got_q, got_w, len_out, len_in, e_loc, give, back,
    in_sem, kv_sem, in_dp, in_h, h_send, h_recv, q_send, q_recv, w_send, w_recv, b_send, b_recv,
):
    me, head = lax.axis_index("dp"), lax.axis_index("heads")

    barrier = pltpu.get_barrier_semaphore()

    @pl.loop(me + 1, n_dp)
    def _(d):
        pl.semaphore_signal(barrier, inc=1, device_id={"dp": d}, device_id_type=MESH)

    @pl.loop(head + 1, n_heads)
    def _(h):
        pl.semaphore_signal(barrier, inc=1, device_id={"heads": h}, device_id_type=MESH)

    small = [
        pltpu.make_async_copy(src, dst, in_sem.at[i])
        for i, (src, dst) in enumerate(
            [(seen_hbm, seen_ref), (plan_hbm, plan_ref), (table_hbm, table_ref),
             (q_hbm, q_ref), (table_hbm, table_s), (fin_hbm, fin_ref)]
        )
    ]
    for c in small:
        c.start()
    k_copy = pltpu.make_async_copy(k_hbm, k_buf, kv_sem.at[0])
    v_copy = pltpu.make_async_copy(v_hbm, v_buf, kv_sem.at[1])
    k_copy.start()
    v_copy.start()

    @pl.when(me + head > 0)
    def _():
        pl.semaphore_wait(barrier, me + head)

    @pl.loop(0, me)
    def _(d):
        pl.semaphore_signal(in_dp.at[me], inc=1, device_id={"dp": d}, device_id_type=MESH)

    @pl.loop(0, head)
    def _(h):
        pl.semaphore_signal(in_h.at[head], inc=1, device_id={"heads": h}, device_id_type=MESH)

    def h_copy(h):
        return pltpu.make_async_remote_copy(
            src_ref=len_out, dst_ref=len_in.at[head],
            send_sem=h_send.at[h], recv_sem=h_recv.at[head],
            device_id={"heads": h}, device_id_type=MESH,
        )

    def h_arrival(h):
        return pltpu.make_async_remote_copy(
            src_ref=len_out, dst_ref=len_in.at[h],
            send_sem=h_send.at[h], recv_sem=h_recv.at[h],
            device_id={"heads": h}, device_id_type=MESH,
        )

    for c in small:
        c.wait()
    len_out[...] = jnp.zeros((1, 128), I32)
    len_out[0:1, 0:8] = seen_ref[...]
    len_in[head] = len_out[...]

    @pl.loop(0, n_heads)
    def _(h):
        @pl.when(h > head)
        def _():
            pl.semaphore_wait(in_h.at[h], 1)

        @pl.when(h != head)
        def _():
            h_copy(h).start()

    src, slot, dest = plan_ref[0:1, :].astype(F32), plan_ref[1:2, :].astype(F32), plan_ref[2:3, :]
    rows = src.shape[1]
    sub, lane = iota((rows, rows), 0), iota((rows, rows), 1)
    src_col = jnp.sum(jnp.where(sub == lane, src, 0.0), axis=1, keepdims=True)
    same = (src_col == src) & (sub < lane)
    rank = jnp.sum(jnp.where(same, 1.0, 0.0), axis=0, keepdims=True)
    place = src * 2.0 + rank
    sub8 = iota((8, rows), 0)
    entry = jnp.zeros((8, rows), F32)
    for t in range(8):
        hit = table_ref[:, t : t + 1] == dest
        entry = entry + jnp.where(hit, (sub8 * 8 + t).astype(F32), 0.0)
    entry = jnp.sum(entry, axis=0, keepdims=True)
    session = jnp.floor(entry * 0.125)
    page = entry - session * 8.0

    row16 = iota((16, rows), 0) // 2
    hot16f = jnp.where(row16.astype(F32) == session, 1.0, 0.0)
    hot16 = hot16f.astype(BF16)
    n_back = n_dp * 8
    r8 = iota((n_back, rows), 0)
    spread = one_hot((r8 // 8 * 2 + (r8 % 8 // 2) % 2).astype(F32) == place)
    pick = nt(spread, hot16)
    row_a, col_a = iota((n_back, 16), 0), iota((n_back, 16), 1)
    pick = jnp.where((row_a % 2 == col_a % 2) & (row_a % 8 < 4), pick, 0.0).astype(BF16)
    q16 = q_ref[...].astype(F32).reshape(16, 128).astype(BF16)
    ask_q[...] = nn(pick, q16).reshape(n_dp, 8, 128).astype(BF16)
    at = one_hot(iota((n_dp, rows), 0).astype(F32) == src)
    mine_w = iota((128, rows), 0).astype(F32) == rank
    slot_part = nt(at, jnp.where(mine_w, slot, 0.0).astype(BF16))

    take = nt(hot16, spread)
    row_b, col_b = iota((16, n_back), 0), iota((16, n_back), 1)
    fits = row_b % 2 == col_b % 2
    take_num = jnp.where(fits & (col_b % 8 < 4), take, 0.0).astype(BF16)
    take_den = jnp.where(fits & (col_b % 8 >= 4), take, 0.0).astype(BF16)
    back[me] = jnp.zeros((8, 128), BF16)
    moved = [
        jnp.sum(jnp.where(page == float(t), hot16f, 0.0), axis=1, keepdims=True) for t in range(8)
    ]

    @pl.loop(0, n_heads)
    def _(h):
        @pl.when(h != head)
        def _():
            h_arrival(h).wait_recv()

    lengths = jnp.max(len_in[...], axis=0).astype(F32)
    r16, l16 = iota((16, 128), 0) // 2, iota((16, 128), 1)
    len_col = jnp.sum(jnp.where(r16 == l16, lengths, 0.0), axis=1, keepdims=True)
    row_len = jnp.sum(hot16f * len_col, axis=0, keepdims=True) * 0.5
    live = jnp.clip(row_len - 256.0 * page, 0.0, 256.0)
    live_part = nt(at, jnp.where(mine_w, live, 0.0).astype(BF16))
    ask_w[...] = (slot_part + 64.0 * live_part).astype(I32).reshape(n_dp, 1, 128)

    def q_copy(d, slot_at):
        return pltpu.make_async_remote_copy(
            src_ref=ask_q.at[d], dst_ref=got_q.at[slot_at],
            send_sem=q_send.at[d], recv_sem=q_recv.at[slot_at],
            device_id={"dp": d}, device_id_type=MESH,
        )

    def w_copy(d, slot_at):
        return pltpu.make_async_remote_copy(
            src_ref=ask_w.at[d], dst_ref=got_w.at[slot_at],
            send_sem=w_send.at[d], recv_sem=w_recv.at[slot_at],
            device_id={"dp": d}, device_id_type=MESH,
        )

    def b_copy(d, slot_at):
        return pltpu.make_async_remote_copy(
            src_ref=give.at[d], dst_ref=back.at[slot_at],
            send_sem=b_send.at[d], recv_sem=b_recv.at[slot_at],
            device_id={"dp": d}, device_id_type=MESH,
        )

    @pl.loop(0, n_dp)
    def _(d):
        @pl.when(d > me)
        def _():
            pl.semaphore_wait(in_dp.at[d], 1)

        @pl.when(d != me)
        def _():
            w_copy(d, me).start()
            q_copy(d, me).start()

    got_q[me] = jnp.zeros((8, 128), BF16)
    got_w[me] = jnp.zeros((1, 128), I32)

    row_q = iota((16, 128), 0) // 2
    k_copy.wait()
    q16f = q16.astype(F32)
    for t in range(8):
        s = jnp.zeros((16, 256), F32)
        for n in range(8):
            s = s + nt(jnp.where(row_q == n, q16f, 0.0).astype(BF16), k_buf[table_s[n, t]])
        e_loc[t] = weights(s)
    tok16 = iota((16, 256), 1).astype(F32)
    row_w = iota((16, 256), 0) // 2
    num = jnp.zeros((16, 128), F32)
    den = jnp.zeros((16, 256), F32)
    v_copy.wait()
    for t in range(8):
        limit = jnp.where(moved[t] > 0.0, 0.0, len_col - 256.0 * t)
        w = jnp.where(tok16 < limit, e_loc[t], 0.0).astype(BF16).astype(F32)
        den = den + w
        for n in range(8):
            num = num + nn(jnp.where(row_w == n, w, 0.0).astype(BF16), v_buf[table_s[n, t]])
    den = jnp.sum(den, axis=1, keepdims=True)

    row8, row8w = iota((8, 128), 0), iota((8, 256), 0)
    tok8 = iota((8, 256), 1)

    @pl.loop(0, n_dp // BATCH)
    def _(i):
        held = []
        for j in range(BATCH):
            d = i * BATCH + j

            @pl.when(d != me)
            def _():
                w_copy(d, d).wait_recv()
                q_copy(d, d).wait_recv()

        for j in range(BATCH):
            d = i * BATCH + j
            q8 = got_q[d].astype(F32)
            words = got_w[d]
            a, b = words[0, 0], words[0, 1]
            s = nt(jnp.where(row8 < 2, q8, 0.0).astype(BF16), k_buf[a & 63])
            s = s + nt(jnp.where(row8 >= 2, q8, 0.0).astype(BF16), k_buf[b & 63])
            held.append((d, a, b, s))
        for d, a, b, s in held:
            limit = jnp.where(row8w < 2, a >> 6, b >> 6)
            w = jnp.where(tok8 < limit, weights(s), 0.0).astype(BF16).astype(F32)
            m = nn(jnp.where(row8w < 2, w, 0.0).astype(BF16), v_buf[a & 63])
            m = m + nn(jnp.where(row8w >= 2, w, 0.0).astype(BF16), v_buf[b & 63])
            total = jnp.broadcast_to(jnp.sum(w, axis=1, keepdims=True), (8, 128))
            give[d] = jnp.where(row8 < 4, m, pltpu.roll(total, 4, 0)).astype(BF16)
        for j in range(BATCH):
            d = i * BATCH + j

            @pl.when(d != me)
            def _():
                b_copy(d, me).start()

    @pl.loop(0, n_dp)
    def _(d):
        @pl.when(d != me)
        def _():
            b_copy(d, d).wait_recv()

    got = back[...].astype(F32).reshape(n_back, 128).astype(BF16)
    num = num + nn(take_num, got)
    den = den + nn(take_den, got)
    ended = jnp.concatenate([fin_ref[...].astype(F32), jnp.zeros((1, 120), F32)], axis=1)
    ended = jnp.sum(jnp.where(r16 == l16, ended, 0.0), axis=1, keepdims=True)
    out_ref[...] = jnp.where(ended == 1.0, 0.0, num / den).astype(BF16)

    @pl.loop(0, n_heads)
    def _(h):
        @pl.when(h != head)
        def _():
            h_copy(h).wait_send()

    @pl.loop(0, n_dp)
    def _(d):
        @pl.when(d != me)
        def _():
            w_copy(d, me).wait_send()
            q_copy(d, me).wait_send()
            b_copy(d, me).wait_send()


def body(queries, key_cache, value_cache, lengths_seen, page_table, finished, move_plan):
    n_dp, n_heads = lax.axis_size("dp"), lax.axis_size("heads")
    slots, _, page, dim = key_cache.shape
    sessions, group, _ = queries.shape
    moves = move_plan.shape[0]
    hbm = pl.BlockSpec(memory_space=pltpu.HBM)
    dma, regular = pltpu.SemaphoreType.DMA, pltpu.SemaphoreType.REGULAR
    vmem = pltpu.VMEM
    out = pl.pallas_call(
        functools.partial(kernel, n_dp, n_heads),
        out_shape=jax.ShapeDtypeStruct((sessions * group, dim), BF16),
        in_specs=[hbm] * 7,
        out_specs=pl.BlockSpec(memory_space=pltpu.VMEM),
        scratch_shapes=[
            vmem((sessions, group, dim), BF16),
            vmem((slots, page, dim), BF16),
            vmem((slots, page, dim), BF16),
            vmem((1, sessions), I32),
            pltpu.SMEM(page_table.shape, I32),
            vmem(page_table.shape, I32),
            vmem((1, sessions), I32),
            vmem((3, moves), I32),
            vmem((n_dp, 8, dim), BF16),
            vmem((n_dp, 1, 128), I32),
            vmem((n_dp, 8, dim), BF16),
            vmem((n_dp, 1, 128), I32),
            vmem((1, 128), I32),
            vmem((n_heads, 1, 128), I32),
            vmem((8, 16, page), F32),
            vmem((n_dp, 8, dim), BF16),
            vmem((n_dp, 8, dim), BF16),
            dma((6,)), dma((2,)),
            regular((n_dp,)), regular((n_heads,)),
            dma((n_heads,)), dma((n_heads,)),
            dma((n_dp,)), dma((n_dp,)),
            dma((n_dp,)), dma((n_dp,)),
            dma((n_dp,)), dma((n_dp,)),
        ],
        compiler_params=pltpu.CompilerParams(
            collective_id=0, has_side_effects=True, vmem_limit_bytes=67043328
        ),
        name="attend",
    )(
        queries,
        key_cache.reshape(slots, page, dim),
        value_cache.reshape(slots, page, dim),
        lengths_seen.reshape(1, sessions),
        page_table,
        finished.reshape(1, sessions),
        move_plan.T,
    )
    return out.reshape(sessions, group, dim)


def solution(mesh):
    in_specs = (
        P("dp", "heads", None),
        P("dp", "heads", None, None),
        P("dp", "heads", None, None),
        P("dp", "heads"),
        P("dp", None),
        P("dp"),
        P("dp", None),
    )
    out_specs = P("dp", "heads", None)
    return jax.shard_map(body, mesh=mesh, in_specs=in_specs, out_specs=out_specs, check_vma=False)
```

time: 45.7 us -> 27.8 us (0.61)
  the two profiles are of different devices: /device:TPU:1 before, /device:TPU:24 now
where the time goes in v2:
time: 27.8 us; the launch traced here: 27.6 us
  Pallas kernels  26.4 us (95%)
  local copies, waits for them, and re-layouts  1.28 us (5%)
    pallas_call x1, Pallas kernels, body(): pl.pallas_call(functools.partial(kernel, n_dp, n_heads), out_shape=jax.Sh...  26.4 us
    unnamed x1, local copies, waits for them, and re-layouts  1.28 us

profile of v2, /device:TPU:24, one launch (start us, length us, event | category | flops | bytes accessed | tf_op | source)
XLA Modules:
  0.0 27.6 jit_solution(11303757394661075297)
XLA Ops:
  0.0 26.4 %attend.1 = bf16[16,128]{1,0:T(8,128)(2,1)} custom-call(bf16[8,2,128]{2,1,0:T(2,128)(2,1)} %q_hbm.1, bf16[64,256,128]{2,1,0:T(8,128)(2,1)} %bitcast.6, bf16[64,256,128]{2,1,0:T(8,128)(2,1)} %bitcast.7, s32[1,8]{1,0:T(1,128)} %bitcast.10, s32[8,8]{1,0:T(8,128)} %table_hbm.1, s32[1,8]{1,0:T(1,128)} %bitcast.11, s32[3,32]{1,0:T(4,128)} %bitcast.9), custom_call_target="tpu_custom_call" | custom-call | tf_op jit(solution)/shard_map/attend/pallas_call | solution.py:298
  26.4 1.3 %copy.9 = bf16[8,2,128]{2,1,0:T(2,128)(2,1)} copy(bf16[8,2,128]{2,1,0:T(2,128)(2,1)} %bitcast.8) | data formatting | bytes 8192

commit v3 on v2

--- a/solution.py
+++ b/solution.py
@@ -9,7 +9,7 @@
 
 MESH = pl.DeviceIdType.MESH
 F32, BF16, I32 = jnp.float32, jnp.bfloat16, jnp.int32
-BATCH = 4
+NZ, NX = 8, 4
 
 
 def nt(a, b, precision=None):
@@ -26,6 +26,10 @@
 
 def iota(shape, dim):
     return lax.broadcasted_iota(I32, shape, dim)
+
+
+def swap(h):
+    return h + 1 - 2 * (h % 2)
 
 
 def one_hot(mask):
@@ -41,20 +45,38 @@
     q_hbm, k_hbm, v_hbm, seen_hbm, table_hbm, fin_hbm, plan_hbm,
     out_ref,
     q_ref, k_buf, v_buf, seen_ref, table_s, table_ref, fin_ref, plan_ref,
-    ask_q, ask_w, got_q, got_w, len_out, len_in, e_loc, give, back,
-    in_sem, kv_sem, in_dp, in_h, h_send, h_recv, q_send, q_recv, w_send, w_recv, b_send, b_recv,
+    ask_q, ask_w, mid_q, mid_w, got_q, got_w, len_out, len_in, e_loc, give, back,
+    in_sem, kv_sem, in_z, in_x, in_h, in_all, h_send, h_recv,
+    xq_send, xq_recv, xw_send, xw_recv, zq_send, zq_recv, zw_send, zw_recv, b_send, b_recv,
 ):
     me, head = lax.axis_index("dp"), lax.axis_index("heads")
+    mz, mx = me // NX, me % NX
+
+    def at_z(z):
+        return {"dp": z * NX + mx}
+
+    def at_x(x):
+        return {"dp": mz * NX + x}
+
+    half = NZ // 2
+    early = mz < half
+    rank_h = swap(head)
 
     barrier = pltpu.get_barrier_semaphore()
 
-    @pl.loop(me + 1, n_dp)
-    def _(d):
-        pl.semaphore_signal(barrier, inc=1, device_id={"dp": d}, device_id_type=MESH)
-
-    @pl.loop(head + 1, n_heads)
-    def _(h):
-        pl.semaphore_signal(barrier, inc=1, device_id={"heads": h}, device_id_type=MESH)
+    @pl.when(early)
+    def _():
+        @pl.loop(mz + 1, NZ)
+        def _(z):
+            pl.semaphore_signal(barrier, inc=1, device_id=at_z(z), device_id_type=MESH)
+
+    @pl.loop(mx + 1, NX)
+    def _(x):
+        pl.semaphore_signal(barrier, inc=1, device_id=at_x(x), device_id_type=MESH)
+
+    @pl.loop(rank_h + 1, n_heads)
+    def _(r):
+        pl.semaphore_signal(barrier, inc=1, device_id={"heads": swap(r)}, device_id_type=MESH)
 
     small = [
         pltpu.make_async_copy(src, dst, in_sem.at[i])
@@ -70,17 +92,23 @@
     k_copy.start()
     v_copy.start()
 
-    @pl.when(me + head > 0)
+    before = jnp.where(early, mz, half)
+
+    @pl.when(before + mx + rank_h > 0)
     def _():
-        pl.semaphore_wait(barrier, me + head)
-
-    @pl.loop(0, me)
-    def _(d):
-        pl.semaphore_signal(in_dp.at[me], inc=1, device_id={"dp": d}, device_id_type=MESH)
-
-    @pl.loop(0, head)
-    def _(h):
-        pl.semaphore_signal(in_h.at[head], inc=1, device_id={"heads": h}, device_id_type=MESH)
+        pl.semaphore_wait(barrier, before + mx + rank_h)
+
+    @pl.loop(0, before)
+    def _(z):
+        pl.semaphore_signal(in_z.at[mz], inc=1, device_id=at_z(z), device_id_type=MESH)
+
+    @pl.loop(0, rank_h)
+    def _(r):
+        pl.semaphore_signal(in_h.at[head], inc=1, device_id={"heads": swap(r)}, device_id_type=MESH)
+
+    @pl.loop(0, mx)
+    def _(x):
+        pl.semaphore_signal(in_x.at[mx], inc=1, device_id=at_x(x), device_id_type=MESH)
 
     def h_copy(h):
         return pltpu.make_async_remote_copy(
@@ -96,24 +124,60 @@
             device_id={"heads": h}, device_id_type=MESH,
         )
 
-    for c in small:
-        c.wait()
+    small[0].wait()
     len_out[...] = jnp.zeros((1, 128), I32)
     len_out[0:1, 0:8] = seen_ref[...]
     len_in[head] = len_out[...]
 
     @pl.loop(0, n_heads)
-    def _(h):
-        @pl.when(h > head)
+    def _(r):
+        h = swap(r)
+
+        @pl.when(r > rank_h)
         def _():
             pl.semaphore_wait(in_h.at[h], 1)
 
-        @pl.when(h != head)
+        @pl.when(r != rank_h)
         def _():
             h_copy(h).start()
+
+    for c in small[1:]:
+        c.wait()
+
+    def x_copy(src, dst, send, recv, x, x_from):
+        return pltpu.make_async_remote_copy(
+            src_ref=src.at[x], dst_ref=dst.at[x_from], send_sem=send.at[x], recv_sem=recv.at[x_from],
+            device_id=at_x(x), device_id_type=MESH,
+        )
+
+    def z_copy(src, dst, send, recv, z, z_from):
+        return pltpu.make_async_remote_copy(
+            src_ref=src.at[:, z], dst_ref=dst.at[z_from], send_sem=send.at[z], recv_sem=recv.at[z_from],
+            device_id=at_z(z), device_id_type=MESH,
+        )
+
+    def xq_copy(x, x_from):
+        return x_copy(ask_q, mid_q, xq_send, xq_recv, x, x_from)
+
+    def xw_copy(x, x_from):
+        return x_copy(ask_w, mid_w, xw_send, xw_recv, x, x_from)
+
+    def zq_copy(z, z_from):
+        return z_copy(mid_q, got_q, zq_send, zq_recv, z, z_from)
+
+    def zw_copy(z, z_from):
+        return z_copy(mid_w, got_w, zw_send, zw_recv, z, z_from)
+
+    def b_copy(d, place_at):
+        return pltpu.make_async_remote_copy(
+            src_ref=give.at[d], dst_ref=back.at[place_at], send_sem=b_send.at[d], recv_sem=b_recv.at[place_at],
+            device_id={"dp": d}, device_id_type=MESH,
+        )
 
     src, slot, dest = plan_ref[0:1, :].astype(F32), plan_ref[1:2, :].astype(F32), plan_ref[2:3, :]
     rows = src.shape[1]
+    src_z = jnp.floor(src / NX)
+    src = (src - NX * src_z) * NZ + src_z
     sub, lane = iota((rows, rows), 0), iota((rows, rows), 1)
     src_col = jnp.sum(jnp.where(sub == lane, src, 0.0), axis=1, keepdims=True)
     same = (src_col == src) & (sub < lane)
@@ -138,7 +202,19 @@
     row_a, col_a = iota((n_back, 16), 0), iota((n_back, 16), 1)
     pick = jnp.where((row_a % 2 == col_a % 2) & (row_a % 8 < 4), pick, 0.0).astype(BF16)
     q16 = q_ref[...].astype(F32).reshape(16, 128).astype(BF16)
-    ask_q[...] = nn(pick, q16).reshape(n_dp, 8, 128).astype(BF16)
+    ask_q[...] = nn(pick, q16).reshape(NX, NZ, 8, 128).astype(BF16)
+    mid_q[mx] = ask_q[mx]
+
+    @pl.loop(0, NX)
+    def _(x):
+        @pl.when(x > mx)
+        def _():
+            pl.semaphore_wait(in_x.at[x], 1)
+
+        @pl.when(x != mx)
+        def _():
+            xq_copy(x, mx).start()
+
     at = one_hot(iota((n_dp, rows), 0).astype(F32) == src)
     mine_w = iota((128, rows), 0).astype(F32) == rank
     slot_part = nt(at, jnp.where(mine_w, slot, 0.0).astype(BF16))
@@ -148,7 +224,7 @@
     fits = row_b % 2 == col_b % 2
     take_num = jnp.where(fits & (col_b % 8 < 4), take, 0.0).astype(BF16)
     take_den = jnp.where(fits & (col_b % 8 >= 4), take, 0.0).astype(BF16)
-    back[me] = jnp.zeros((8, 128), BF16)
+    back[mx * NZ + mz] = jnp.zeros((8, 128), BF16)
     moved = [
         jnp.sum(jnp.where(page == float(t), hot16f, 0.0), axis=1, keepdims=True) for t in range(8)
     ]
@@ -165,42 +241,15 @@
     row_len = jnp.sum(hot16f * len_col, axis=0, keepdims=True) * 0.5
     live = jnp.clip(row_len - 256.0 * page, 0.0, 256.0)
     live_part = nt(at, jnp.where(mine_w, live, 0.0).astype(BF16))
-    ask_w[...] = (slot_part + 64.0 * live_part).astype(I32).reshape(n_dp, 1, 128)
-
-    def q_copy(d, slot_at):
-        return pltpu.make_async_remote_copy(
-            src_ref=ask_q.at[d], dst_ref=got_q.at[slot_at],
-            send_sem=q_send.at[d], recv_sem=q_recv.at[slot_at],
-            device_id={"dp": d}, device_id_type=MESH,
-        )
-
-    def w_copy(d, slot_at):
-        return pltpu.make_async_remote_copy(
-            src_ref=ask_w.at[d], dst_ref=got_w.at[slot_at],
-            send_sem=w_send.at[d], recv_sem=w_recv.at[slot_at],
-            device_id={"dp": d}, device_id_type=MESH,
-        )
-
-    def b_copy(d, slot_at):
-        return pltpu.make_async_remote_copy(
-            src_ref=give.at[d], dst_ref=back.at[slot_at],
-            send_sem=b_send.at[d], recv_sem=b_recv.at[slot_at],
-            device_id={"dp": d}, device_id_type=MESH,
-        )
-
-    @pl.loop(0, n_dp)
-    def _(d):
-        @pl.when(d > me)
-        def _():
-            pl.semaphore_wait(in_dp.at[d], 1)
-
-        @pl.when(d != me)
-        def _():
-            w_copy(d, me).start()
-            q_copy(d, me).start()
-
-    got_q[me] = jnp.zeros((8, 128), BF16)
-    got_w[me] = jnp.zeros((1, 128), I32)
+    ask_w[...] = (slot_part + 64.0 * live_part).astype(I32).reshape(NX, NZ, 1, 128)
+
+    mid_w[mx] = ask_w[mx]
+
+    @pl.loop(0, NX)
+    def _(x):
+        @pl.when(x != mx)
+        def _():
+            xw_copy(x, mx).start()
 
     row_q = iota((16, 128), 0) // 2
     k_copy.wait()
@@ -223,28 +272,54 @@
             num = num + nn(jnp.where(row_w == n, w, 0.0).astype(BF16), v_buf[table_s[n, t]])
     den = jnp.sum(den, axis=1, keepdims=True)
 
+    @pl.loop(0, NX)
+    def _(x):
+        @pl.when(x != mx)
+        def _():
+            xq_copy(x, x).wait_recv()
+            xw_copy(x, x).wait_recv()
+
+    @pl.loop(0, NZ)
+    def _(z):
+        @pl.when(early & (z > mz))
+        def _():
+            pl.semaphore_wait(in_z.at[z], 1)
+
+        @pl.when((mz >= half) & (z == half))
+        def _():
+            pl.semaphore_wait(in_all, 1)
+
+        @pl.when(z != mz)
+        def _():
+            zw_copy(z, mz).start()
+            zq_copy(z, mz).start()
+
+    @pl.when(early)
+    def _():
+        pl.semaphore_signal(in_all, inc=1, device_id=at_z(NZ - 1 - mz), device_id_type=MESH)
+
+    for x in range(NX):
+        got_q[mz, x] = mid_q[x, mz]
+        got_w[mz, x] = mid_w[x, mz]
+
     row8, row8w = iota((8, 128), 0), iota((8, 256), 0)
     tok8 = iota((8, 256), 1)
 
-    @pl.loop(0, n_dp // BATCH)
-    def _(i):
+    @pl.loop(0, NZ)
+    def _(z):
+        @pl.when(z != mz)
+        def _():
+            zw_copy(z, z).wait_recv()
+            zq_copy(z, z).wait_recv()
+
         held = []
-        for j in range(BATCH):
-            d = i * BATCH + j
-
-            @pl.when(d != me)
-            def _():
-                w_copy(d, d).wait_recv()
-                q_copy(d, d).wait_recv()
-
-        for j in range(BATCH):
-            d = i * BATCH + j
-            q8 = got_q[d].astype(F32)
-            words = got_w[d]
+        for x in range(NX):
+            q8 = got_q[z, x].astype(F32)
+            words = got_w[z, x]
             a, b = words[0, 0], words[0, 1]
             s = nt(jnp.where(row8 < 2, q8, 0.0).astype(BF16), k_buf[a & 63])
             s = s + nt(jnp.where(row8 >= 2, q8, 0.0).astype(BF16), k_buf[b & 63])
-            held.append((d, a, b, s))
+            held.append((z * NX + x, a, b, s))
         for d, a, b, s in held:
             limit = jnp.where(row8w < 2, a >> 6, b >> 6)
             w = jnp.where(tok8 < limit, weights(s), 0.0).astype(BF16).astype(F32)
@@ -252,18 +327,18 @@
             m = m + nn(jnp.where(row8w >= 2, w, 0.0).astype(BF16), v_buf[b & 63])
             total = jnp.broadcast_to(jnp.sum(w, axis=1, keepdims=True), (8, 128))
             give[d] = jnp.where(row8 < 4, m, pltpu.roll(total, 4, 0)).astype(BF16)
-        for j in range(BATCH):
-            d = i * BATCH + j
+        for x in range(NX):
+            d = z * NX + x
 
             @pl.when(d != me)
             def _():
-                b_copy(d, me).start()
+                b_copy(d, mx * NZ + mz).start()
 
     @pl.loop(0, n_dp)
     def _(d):
         @pl.when(d != me)
         def _():
-            b_copy(d, d).wait_recv()
+            b_copy(d, d % NX * NZ + d // NX).wait_recv()
 
     got = back[...].astype(F32).reshape(n_back, 128).astype(BF16)
     num = num + nn(take_num, got)
@@ -278,12 +353,24 @@
         def _():
             h_copy(h).wait_send()
 
+    @pl.loop(0, NX)
+    def _(x):
+        @pl.when(x != mx)
+        def _():
+            xq_copy(x, mx).wait_send()
+            xw_copy(x, mx).wait_send()
+
+    @pl.loop(0, NZ)
+    def _(z):
+        @pl.when(z != mz)
+        def _():
+            zq_copy(z, mz).wait_send()
+            zw_copy(z, mz).wait_send()
+
     @pl.loop(0, n_dp)
     def _(d):
         @pl.when(d != me)
         def _():
-            w_copy(d, me).wait_send()
-            q_copy(d, me).wait_send()
             b_copy(d, me).wait_send()
 
 
@@ -297,7 +384,7 @@
     vmem = pltpu.VMEM
     out = pl.pallas_call(
         functools.partial(kernel, n_dp, n_heads),
-        out_shape=jax.ShapeDtypeStruct((sessions * group, dim), BF16),
+        out_shape=vmem((sessions * group, dim), BF16),
         in_specs=[hbm] * 7,
         out_specs=pl.BlockSpec(memory_space=pltpu.VMEM),
         scratch_shapes=[
@@ -309,27 +396,29 @@
             vmem(page_table.shape, I32),
             vmem((1, sessions), I32),
             vmem((3, moves), I32),
-            vmem((n_dp, 8, dim), BF16),
-            vmem((n_dp, 1, 128), I32),
-            vmem((n_dp, 8, dim), BF16),
-            vmem((n_dp, 1, 128), I32),
+            vmem((NX, NZ, 8, dim), BF16),
+            vmem((NX, NZ, 1, 128), I32),
+            vmem((NX, NZ, 8, dim), BF16),
+            vmem((NX, NZ, 1, 128), I32),
+            vmem((NZ, NX, 8, dim), BF16),
+            vmem((NZ, NX, 1, 128), I32),
             vmem((1, 128), I32),
             vmem((n_heads, 1, 128), I32),
             vmem((8, 16, page), F32),
             vmem((n_dp, 8, dim), BF16),
             vmem((n_dp, 8, dim), BF16),
             dma((6,)), dma((2,)),
-            regular((n_dp,)), regular((n_heads,)),
+            regular((NZ,)), regular((NX,)), regular((n_heads,)), regular,
             dma((n_heads,)), dma((n_heads,)),
-            dma((n_dp,)), dma((n_dp,)),
-            dma((n_dp,)), dma((n_dp,)),
+            dma((NX,)), dma((NX,)), dma((NX,)), dma((NX,)),
+            dma((NZ,)), dma((NZ,)), dma((NZ,)), dma((NZ,)),
             dma((n_dp,)), dma((n_dp,)),
         ],
         compiler_params=pltpu.CompilerParams(
-            collective_id=0, has_side_effects=True, vmem_limit_bytes=67043328
+            collective_id=0, has_side_effects=True, vmem_limit_bytes=48 << 20
         ),
         name="attend",
-    )(
+    )(*[pltpu.with_memory_space_constraint(a, pltpu.HBM) for a in (
         queries,
         key_cache.reshape(slots, page, dim),
         value_cache.reshape(slots, page, dim),
@@ -337,7 +426,7 @@
         page_table,
         finished.reshape(1, sessions),
         move_plan.T,
-    )
+    )])
     return out.reshape(sessions, group, dim)
 
 

time: 27.8 us -> 25.6 us (0.921)
  the two profiles are of different devices: /device:TPU:24 before, /device:TPU:248 now
where the time goes in v3:
time: 25.6 us; the launch traced here: 25.5 us
  Pallas kernels  24.9 us (97%)
  local copies, waits for them, and re-layouts  0.6 us (2%)
    pallas_call x1, Pallas kernels, body(): pl.pallas_call(functools.partial(kernel, n_dp, n_heads), out_shape=vmem((...  24.9 us
    unnamed x1, local copies, waits for them, and re-layouts  0.6 us

profile of v3, /device:TPU:248, one launch (start us, length us, event | category | flops | bytes accessed | tf_op | source)
XLA Modules:
  0.0 25.5 jit_solution(14826358119142418358)
XLA Ops:
  0.0 24.9 %attend.1 = bf16[16,128]{1,0:T(8,128)(2,1)S(1)} custom-call(bf16[8,2,128]{2,1,0:T(2,128)(2,1)} %q_hbm.1, bf16[64,256,128]{2,1,0:T(8,128)(2,1)} %bitcast.7, bf16[64,256,128]{2,1,0:T(8,128)(2,1)} %bitcast.8, s32[1,8]{1,0:T(1,128)} %bitcast.10, s32[8,8]{1,0:T(8,128)} %table_hbm.1, s32[1,8]{1,0:T(1,128)} %bitcast.11, s32[3,32]{1,0:T(4,128)} %bitcast.9), custom_call_target="tpu_custom_call" | custom-call | tf_op jit(solution)/shard_map/attend/pallas_call | solution.py:385
  24.9 0.6 %copy.9 = bf16[8,2,128]{2,1,0:T(2,128)(2,1)} copy(bf16[8,2,128]{2,1,0:T(2,128)(2,1)S(1)} %bitcast.6) | data formatting | bytes 8192
